TPU v7x, 32 devices: a whole 2x2x4 slice. The times are simulated.
32 devices in a mesh: row: 4 (over z), col: 8 (over y, x, core).
Axes of the slice: x: 2, y: 2, z: 4, core: 2. Of those that a mesh axis runs over, the one named last changes fastest.
Arguments:
- green: float32 [512, 16384], P(('row', 'col')), may hold values from -0.375 to 0.375
- noise_precision: float32 [512], P(('row', 'col')), may hold values from 0.5 to 4
- data_set: int32 [512], P(('row', 'col')), may hold values from 0 to 3
- set_scale: float32 [4], replicated, may hold values from 0.5 to 2
- stiffness: float32 [8192], replicated, may hold values from 0.25 to 2
- patch_cell: int32 [8192], replicated, may hold values from 0 to 8191, each once
Outputs:
- precision_matrix: float32 [16384, 16384], P('row', 'col')
Inputs may be any that keep to these rules, and one draw needn't show every extreme that they name: `patch_cell`: every cell 0 to 8191 holds exactly one patch.
All inputs are finite; a program needn't handle non-finite values.
Results may differ from a plain program's by a relative error of at most 0.00005.
Values sent between devices are 32-bit elements; how exact they have to be, the bound alone decides.
A program may use at most 256 MiB of HBM per device.

v0:
```python
import jax
import jax.numpy as jnp
from jax import lax
from jax.sharding import PartitionSpec as P

NSTRIKE = 128
NDIP = 64


def gram_product(left_panel, right_panel):
    return lax.dot_general(
        left_panel,
        right_panel,
        (((0,), (0,)), ((), ())),
        precision=lax.Precision.HIGHEST,
        preferred_element_type=jnp.float32,
    )


def degree_table(stiffness, patch_cell):
    sorted_cells, cell_stiff = lax.sort_key_val(patch_cell, stiffness)
    grid = cell_stiff.reshape(NSTRIKE, NDIP)
    padded = jnp.pad(grid, 1)
    strike_ids = lax.broadcasted_iota(jnp.int32, (NSTRIKE, NDIP), 0)
    dip_ids = lax.broadcasted_iota(jnp.int32, (NSTRIKE, NDIP), 1)
    degree = jnp.zeros((NSTRIKE, NDIP), jnp.float32)
    degree = degree + jnp.where(strike_ids < NSTRIKE - 1, 0.5 * (grid + padded[2:, 1:-1]), 0.0)
    degree = degree + jnp.where(strike_ids > 0, 0.5 * (grid + padded[:-2, 1:-1]), 0.0)
    degree = degree + jnp.where(dip_ids < NDIP - 1, 0.5 * (grid + padded[1:-1, 2:]), 0.0)
    degree = degree + jnp.where(dip_ids > 0, 0.5 * (grid + padded[1:-1, :-2]), 0.0)
    return degree.reshape(NSTRIKE * NDIP)


def smoothing_tile(stiffness, patch_cell, row_start, tile_height, col_start, tile_width):
    patch_count = stiffness.shape[0]
    degree_cells = degree_table(stiffness, patch_cell)
    row_first = row_start % patch_count
    col_first = col_start % patch_count
    row_cell = lax.dynamic_slice_in_dim(patch_cell, row_first, tile_height, 0)
    col_cell = lax.dynamic_slice_in_dim(patch_cell, col_first, tile_width, 0)
    row_stiff = lax.dynamic_slice_in_dim(stiffness, row_first, tile_height, 0)
    col_stiff = lax.dynamic_slice_in_dim(stiffness, col_first, tile_width, 0)
    row_degree = jnp.take(degree_cells, row_cell)
    row_strike = row_cell // NDIP
    row_dip = row_cell % NDIP
    col_strike = col_cell // NDIP
    col_dip = col_cell % NDIP
    spacing = jnp.abs(row_strike[:, None] - col_strike[None, :]) + jnp.abs(
        row_dip[:, None] - col_dip[None, :]
    )
    row_ids = row_start + jnp.arange(tile_height, dtype=jnp.int32)
    col_ids = col_start + jnp.arange(tile_width, dtype=jnp.int32)
    same_part = row_ids[:, None] // patch_count == col_ids[None, :] // patch_count
    coupling = jnp.where(
        (spacing == 1) & same_part, -0.5 * (row_stiff[:, None] + col_stiff[None, :]), 0.0
    )
    diagonal = row_ids[:, None] == col_ids[None, :]
    return coupling + jnp.where(diagonal, row_degree[:, None], 0.0)


def per_device(green, noise_precision, data_set, set_scale, stiffness, patch_cell):
    row_count = lax.axis_size("row")
    col_count = lax.axis_size("col")
    local_rows = green.shape[0]
    order_full = green.shape[1]
    tile_height = order_full // row_count
    tile_width = order_full // col_count
    matches = data_set[:, None] == jnp.arange(set_scale.shape[0], dtype=jnp.int32)[None, :]
    weight = noise_precision * jnp.sum(jnp.where(matches, set_scale[None, :], 0.0), axis=1)
    scaled = green * jnp.sqrt(weight)[:, None]
    by_column = lax.all_to_all(scaled, "col", split_axis=1, concat_axis=0, tiled=True)
    right_factor = lax.all_gather(by_column, "row", axis=0, tiled=True)
    by_row = lax.all_to_all(scaled, "row", split_axis=1, concat_axis=0, tiled=True)
    reordered = jnp.transpose(
        right_factor.reshape(row_count, col_count, local_rows, tile_width), (1, 0, 2, 3)
    ).reshape(row_count * col_count * local_rows, tile_width)
    gram_tile = gram_product(lax.all_gather(by_row, "col", axis=0, tiled=True), reordered)
    prior = smoothing_tile(
        stiffness,
        patch_cell,
        lax.axis_index("row") * tile_height,
        tile_height,
        lax.axis_index("col") * tile_width,
        tile_width,
    )
    return gram_tile + prior


def solution(mesh):
    placed = (P(("row", "col"), None), P(("row", "col")), P(("row", "col")), P(), P(), P())
    return jax.shard_map(
        per_device, mesh=mesh, in_specs=placed, out_specs=P("row", "col"), check_vma=False
    )
```

profile of v0, /device:TPU:0, one launch (start us, length us, event | category | flops | bytes accessed | tf_op | source)
XLA Modules:
  0.0 266.4 jit_solution(3653453270997233853)
XLA Ops:
  6.5 0.8 select_reduce_fusion
  7.3 0.7 multiply_sqrt_fusion
  8.0 1.4 broadcast_multiply_fusion
  9.3 0.1 copy.21
  9.4 20.4 %all_to_all.38 = f32[16,8,2048]{2,0,1:T(8,128)} all-to-all(f32[16,8,2048]{2,0,1:T(8,128)S(1)} %bitcast.27), channel_id=1, replica_groups=mesh['row'=4,'col'=8] {'col'}, dimensions={1} | all-to-all | bytes 2097152 | tf_op jit(solution)/shard_map/all_to_all | solution.py:71
  29.9 0.0 all-gather.3.cloned.1.call-start
  29.9 0.1 copy.22
  30.0 57.1 %all_to_all.39 = f32[16,4,4096]{2,0,1:T(8,128)} all-to-all(f32[16,4,4096]{2,0,1:T(8,128)S(1)} %bitcast.26), channel_id=1, replica_groups=mesh['row'=4,'col'=8] {'row'}, dimensions={1} | all-to-all | bytes 2097152 | tf_op jit(solution)/shard_map/all_to_all | solution.py:73
  87.1 0.7 dynamic_slice.15
  87.8 0.7 dynamic_slice.14
  88.6 7.7 %sort.23 = (s32[8192]{0:T(1024)}, f32[8192]{0:T(1024)S(1)}, s32[8192]{0:T(1024)}) sort(s32[8192]{0:T(1024)} %param.11, f32[8192]{0:T(1024)} %param.10, s32[8192]{0:T(1024)S(1)} %iota.45), dimensions={0}, to_apply=%region_1.2 | sort | flops 106496 | bytes 196608 | tf_op jit(solution)/shard_map/sort | solution.py:21
  96.2 0.1 reshape.114
  96.3 0.1 select_add_fusion
  96.5 0.1 reshape.115
  96.5 0.7 add_select_fusion.3
  97.3 0.7 add_select_fusion.2
  98.0 23.0 %gather_fusion = f32[4096]{0:T(1024)S(1)} fusion(f32[8192]{0:T(1024)S(1)} %reshape.115, s32[4096]{0:T(1024)S(1)} %get-tuple-element.14), kind=kCustom, calls=%fused_computation | custom fusion | bytes 49152 | tf_op jit(solution)/shard_map/jit(_take)/gather | solution.py:43
  121.1 0.7 add_select_fusion.6
  121.8 0.7 add_select_fusion.5
  122.5 0.7 and_select_fusion
  123.3 4.5 %all-gather.5.cloned.1.call-done = f32[512,2048]{1,0:T(8,128)} async-done(((f32[128,2048]{1,0:T(8,128)}), f32[512,2048]{1,0:T(8,128)}) %all-gather.5.cloned.1.call-update) | async-done | bytes 4194320 | tf_op jit(solution)/shard_map/all_gather | solution.py:72
  127.8 4.6 %copy.16 = f32[4,8,16,2048]{3,2,0,1:T(8,128)} copy(f32[4,8,16,2048]{3,2,1,0:T(8,128)} %bitcast.22) | data formatting | bytes 8388608 | tf_op jit(solution)/shard_map/reshape | solution.py:75
  132.4 49.4 %all-gather.3.cloned.1.call-done = f32[512,4096]{1,0:T(8,128)} async-done(((f32[64,4096]{1,0:T(8,128)}), f32[512,4096]{1,0:T(8,128)}) %all-gather.3.cloned.1.call-update) | async-done | bytes 8388624 | tf_op jit(solution)/shard_map/all_gather | solution.py:77
  181.8 77.7 %add_add_fusion = f32[4096,2048]{1,0:T(8,128)} fusion(f32[4096]{0:T(1024)S(1)} %and_select_fusion, s32[2048]{0:T(1024)S(1)} %get-tuple-element.22, f32[2048]{0:T(1024)S(1)} %dynamic_slice.15, f32[4096]{0:T(1024)S(1)} %dynamic_slice.14, s32[2048]{0:T(1024)S(1)} %get-tuple-element.21, s32[2048]{0:T(1024)S(1)} %add_select_fusion.5, ...), kind=kOutput, calls=%fused_computation.1 | convolution fusion | flops 51665436672 | bytes 46276608 | tf_op jit(solution)/shard_map/dot_general | solution.py:11
  (8 shorter events, 0.1 us)
Async XLA Ops:
  6.5 121.2 %all-gather.5.cloned.1.call-start = ((), (), s32[]{:S(2)}) async-start(), calls=%async_computation.3 | async-start | bytes 5242880 | tf_op jit(solution)/shard_map/all_gather | solution.py:72
  29.9 151.9 %all-gather.3.cloned.1.call-start = ((), (), s32[]{:S(2)}) async-start(), calls=%async_computation.2 | async-start | bytes 9437184 | tf_op jit(solution)/shard_map/all_gather | solution.py:77
Sparse Core Ops, SparseCore 0:
  30.0 97.7 all-gather.4
  129.6 52.1 all-gather.2
where the time goes:
time: 267 us; the launch traced here: 266 us
  matrix products  77.7 us (29%)
  blocking collectives  77.5 us (29%)
  waiting for transfers between devices  53.9 us (20%)
  local copies, waits for them, and re-layouts  29.4 us (11%)
  other arithmetic  14.3 us (5%)
  between operations  13.5 us (5%)
    dot_general x1, matrix products, gram_product(): lax.dot_general(left_panel, right_panel, (((0,), (0,)), ((), ())), precis...  77.7 us
    all_to_all x1, blocking collectives, per_device(): lax.all_to_all(scaled, 'row', split_axis=1, concat_axis=0, tiled=True)  57.1 us
    all_gather x1, waiting for transfers between devices, per_device(): lax.all_gather(by_row, 'col', axis=0, tiled=True)  49.4 us
    gather x1, local copies, waits for them, and re-layouts, smoothing_tile(): row_degree = jnp.take(degree_cells, row_cell)  23 us
    all_to_all x1, blocking collectives, per_device(): lax.all_to_all(scaled, 'col', split_axis=1, concat_axis=0, tiled=True)  20.4 us
    sort x1, other arithmetic, degree_table(): sorted_cells, cell_stiff = lax.sort_key_val(patch_cell, stiffness)  7.67 us
  transfers between devices with their start and end apart: 2, of which 2 were waited for; matrix products, arithmetic and copies ran while one was open for 15% of the time, Pallas kernels for 0%

commit v1 on v0

--- a/solution.py
+++ b/solution.py
@@ -1,6 +1,8 @@
 import jax
 import jax.numpy as jnp
 from jax import lax
+from jax.experimental import pallas as pl
+from jax.experimental.pallas import tpu as pltpu
 from jax.sharding import PartitionSpec as P
 
 NSTRIKE = 128
@@ -12,14 +14,26 @@
         left_panel,
         right_panel,
         (((0,), (0,)), ((), ())),
-        precision=lax.Precision.HIGHEST,
+        precision=lax.Precision.HIGH,
         preferred_element_type=jnp.float32,
     )
 
 
+def one_hots(cells):
+    strike_hot = cells[:, None] // NDIP == jnp.arange(NSTRIKE, dtype=jnp.int32)[None, :]
+    dip_hot = cells[:, None] % NDIP == jnp.arange(NDIP, dtype=jnp.int32)[None, :]
+    return strike_hot, dip_hot
+
+
 def degree_table(stiffness, patch_cell):
-    sorted_cells, cell_stiff = lax.sort_key_val(patch_cell, stiffness)
-    grid = cell_stiff.reshape(NSTRIKE, NDIP)
+    strike_hot, dip_hot = one_hots(patch_cell)
+    grid = lax.dot_general(
+        strike_hot.astype(jnp.float32),
+        jnp.where(dip_hot, stiffness[:, None], 0.0),
+        (((0,), (0,)), ((), ())),
+        precision=lax.Precision.HIGHEST,
+        preferred_element_type=jnp.float32,
+    )
     padded = jnp.pad(grid, 1)
     strike_ids = lax.broadcasted_iota(jnp.int32, (NSTRIKE, NDIP), 0)
     dip_ids = lax.broadcasted_iota(jnp.int32, (NSTRIKE, NDIP), 1)
@@ -28,7 +42,18 @@
     degree = degree + jnp.where(strike_ids > 0, 0.5 * (grid + padded[:-2, 1:-1]), 0.0)
     degree = degree + jnp.where(dip_ids < NDIP - 1, 0.5 * (grid + padded[1:-1, 2:]), 0.0)
     degree = degree + jnp.where(dip_ids > 0, 0.5 * (grid + padded[1:-1, :-2]), 0.0)
-    return degree.reshape(NSTRIKE * NDIP)
+    return degree
+
+
+def degree_of(degree, cells):
+    strike_hot, dip_hot = one_hots(cells)
+    lines = jnp.dot(
+        strike_hot.astype(jnp.float32),
+        degree,
+        precision=lax.Precision.HIGHEST,
+        preferred_element_type=jnp.float32,
+    )
+    return jnp.sum(jnp.where(dip_hot, lines, 0.0), axis=1)
 
 
 def smoothing_tile(stiffness, patch_cell, row_start, tile_height, col_start, tile_width):
@@ -40,7 +65,7 @@
     col_cell = lax.dynamic_slice_in_dim(patch_cell, col_first, tile_width, 0)
     row_stiff = lax.dynamic_slice_in_dim(stiffness, row_first, tile_height, 0)
     col_stiff = lax.dynamic_slice_in_dim(stiffness, col_first, tile_width, 0)
-    row_degree = jnp.take(degree_cells, row_cell)
+    row_degree = degree_of(degree_cells, row_cell)
     row_strike = row_cell // NDIP
     row_dip = row_cell % NDIP
     col_strike = col_cell // NDIP
@@ -58,6 +83,80 @@
     return coupling + jnp.where(diagonal, row_degree[:, None], 0.0)
 
 
+def exchange_kernel(row_count, col_count, block, by_row, by_column, send, recv, own):
+    row = lax.axis_index("row")
+    col = lax.axis_index("col")
+    rows = block.shape[0]
+    height = by_row.shape[1]
+    width = by_column.shape[1]
+    row_slot = by_row.at[pl.ds(pl.multiple_of(row * rows, 8), rows), :]
+    col_slot = by_column.at[pl.ds(pl.multiple_of(col * rows, 8), rows), :]
+    copies = []
+    for step in range(1, row_count):
+        target = lax.rem(row + step, row_count)
+        copies.append(
+            pltpu.make_async_remote_copy(
+                src_ref=block.at[:, pl.ds(pl.multiple_of(target * height, 128), height)],
+                dst_ref=row_slot,
+                send_sem=send.at[step - 1],
+                recv_sem=recv.at[step - 1],
+                device_id=(target, col),
+                device_id_type=pl.DeviceIdType.MESH,
+            )
+        )
+    for step in range(1, col_count):
+        target = lax.rem(col + step, col_count)
+        copies.append(
+            pltpu.make_async_remote_copy(
+                src_ref=block.at[:, pl.ds(pl.multiple_of(target * width, 128), width)],
+                dst_ref=col_slot,
+                send_sem=send.at[row_count + step - 2],
+                recv_sem=recv.at[row_count + step - 2],
+                device_id=(row, target),
+                device_id_type=pl.DeviceIdType.MESH,
+            )
+        )
+    copies.append(
+        pltpu.make_async_copy(
+            block.at[:, pl.ds(pl.multiple_of(row * height, 128), height)], row_slot, own.at[0]
+        )
+    )
+    copies.append(
+        pltpu.make_async_copy(
+            block.at[:, pl.ds(pl.multiple_of(col * width, 128), width)], col_slot, own.at[1]
+        )
+    )
+    for copy in copies:
+        copy.start()
+    for copy in copies:
+        copy.wait()
+
+
+def exchange(scaled, row_count, col_count):
+    rows, order_full = scaled.shape
+    in_vmem = pl.BlockSpec(memory_space=pltpu.VMEM)
+    partners = row_count + col_count - 2
+
+    def body(*refs):
+        exchange_kernel(row_count, col_count, *refs)
+
+    return pl.pallas_call(
+        body,
+        out_shape=(
+            jax.ShapeDtypeStruct((row_count * rows, order_full // row_count), jnp.float32),
+            jax.ShapeDtypeStruct((col_count * rows, order_full // col_count), jnp.float32),
+        ),
+        in_specs=[in_vmem],
+        out_specs=(in_vmem, in_vmem),
+        scratch_shapes=[
+            pltpu.SemaphoreType.DMA((partners,)),
+            pltpu.SemaphoreType.DMA((partners,)),
+            pltpu.SemaphoreType.DMA((2,)),
+        ],
+        compiler_params=pltpu.CompilerParams(has_side_effects=True),
+    )(scaled)
+
+
 def per_device(green, noise_precision, data_set, set_scale, stiffness, patch_cell):
     row_count = lax.axis_size("row")
     col_count = lax.axis_size("col")
@@ -68,9 +167,8 @@
     matches = data_set[:, None] == jnp.arange(set_scale.shape[0], dtype=jnp.int32)[None, :]
     weight = noise_precision * jnp.sum(jnp.where(matches, set_scale[None, :], 0.0), axis=1)
     scaled = green * jnp.sqrt(weight)[:, None]
-    by_column = lax.all_to_all(scaled, "col", split_axis=1, concat_axis=0, tiled=True)
+    by_row, by_column = exchange(scaled, row_count, col_count)
     right_factor = lax.all_gather(by_column, "row", axis=0, tiled=True)
-    by_row = lax.all_to_all(scaled, "row", split_axis=1, concat_axis=0, tiled=True)
     reordered = jnp.transpose(
         right_factor.reshape(row_count, col_count, local_rows, tile_width), (1, 0, 2, 3)
     ).reshape(row_count * col_count * local_rows, tile_width)

time: 267 us -> 240 us (0.90)
  blocking collectives: 77.5 us -> 0 us
  waiting for transfers between devices: 53.9 us -> 125 us
  Pallas kernels: 0 us -> 31.1 us
  local copies, waits for them, and re-layouts: 29.4 us -> 6.04 us
  matrix products: 77.7 us -> 56 us
  other arithmetic: 14.3 us -> 7.48 us
    all_to_all x2 -> x0, blocking collectives: 77.5 us -> none  [the longest x1 57.1 us: per_device(): lax.all_to_all(scaled, 'row', split_axis=1, concat_axis=0, tiled=True)]
    all_gather x1, waiting for transfers between devices: 4.49 us -> 74.6 us  [per_device(): right_factor = lax.all_gather(by_column, 'row', axis=0, tiled=True)]
    pallas_call x0 -> x1, Pallas kernels: none -> 31.1 us  [exchange(): pl.pallas_call(body, out_shape=(jax.ShapeDtypeStruct((row_count * rows, o...]
    dot_general x1, matrix products: 77.7 us -> 51.7 us  [gram_product(): lax.dot_general(left_panel, right_panel, (((0,), (0,)), ((), ())), precis...]
    gather x1 -> x0, local copies, waits for them, and re-layouts: 23 us -> none  [smoothing_tile(): row_degree = jnp.take(degree_cells, row_cell)]
    sort x1 -> x0, other arithmetic: 7.67 us -> none  [degree_table(): sorted_cells, cell_stiff = lax.sort_key_val(patch_cell, stiffness)]
    dot_general x0 -> x2, matrix products: none -> 4.33 us  [the longest x1 2.72 us: degree_table(): lax.dot_general(strike_hot.astype(jnp.float32), jnp.where(dip_hot, stiffn...]
  transfers between devices with their start and end apart: 2 -> 2, of which waited for: 2 -> 2; matrix products, arithmetic and copies ran while one was open for 15% -> 6% of each run, Pallas kernels for 0% -> 0%
where the time goes in v1:
time: 240 us
  waiting for transfers between devices  125 us (52%)
  matrix products  56 us (23%)
  Pallas kernels  31.1 us (13%)
  between operations  13.5 us (6%)
  other arithmetic  7.48 us (3%)
  local copies, waits for them, and re-layouts  6.04 us (3%)
    all_gather x1, waiting for transfers between devices, per_device(): right_factor = lax.all_gather(by_column, 'row', axis=0, tiled=True)  74.6 us
    dot_general x1, matrix products, gram_product(): lax.dot_general(left_panel, right_panel, (((0,), (0,)), ((), ())), precis...  51.7 us
    all_gather x1, waiting for transfers between devices, per_device(): lax.all_gather(by_row, 'col', axis=0, tiled=True)  50 us
    pallas_call x1, Pallas kernels, exchange(): pl.pallas_call(body, out_shape=(jax.ShapeDtypeStruct((row_count * rows, o...  31.1 us
  transfers between devices with their start and end apart: 2, of which 2 were waited for; matrix products, arithmetic and copies ran while one was open for 6% of the time, Pallas kernels for 0%

profile of v1, /device:TPU:0, one launch (start us, length us, event | category | flops | bytes accessed | tf_op | source)
XLA Modules:
  0.0 239.6 jit_solution(9080004859607463196)
XLA Ops:
  6.5 0.0 all-gather.5.cloned.1.call-start
  6.5 0.8 select_reduce_fusion
  7.3 0.7 multiply_sqrt_fusion
  8.0 2.3 broadcast_multiply_fusion.refs_0_
  10.3 31.1 %shard_map.64 = (f32[64,4096]{1,0:T(8,128)}, f32[128,2048]{1,0:T(8,128)}) custom-call(f32[16,16384]{1,0:T(8,128)} %broadcast_multiply_fusion.refs_0_), custom_call_target="tpu_custom_call" | custom-call | tf_op jit(solution)/shard_map/pallas_call | solution.py:143
  41.4 0.0 all-gather.5.cloned.1.call-update
  41.5 0.0 all-gather.3.cloned.1.call-start
  41.5 0.7 all-gather.3.cloned.1.call-update
  42.3 0.7 dynamic_slice.15
  43.0 0.7 dynamic_slice.14
  43.7 0.7 add_select_fusion.7
  44.4 0.7 add_select_fusion.3
  45.2 0.7 add_select_fusion.4
  45.9 0.8 add_select_fusion
  46.7 2.7 %fusion.1 = f32[128,64]{0,1:T(8,128)S(1)} fusion(s32[8192]{0:T(1024)S(1)} %get-tuple-element.14, f32[8192]{0:T(1024)} %param.10, s32[8192]{0:T(1024)S(1)} %get-tuple-element.13), kind=kOutput, calls=%fused_computation.5 | convolution fusion | flops 807403520 | bytes 131072 | tf_op jit(solution)/shard_map/dot_general | solution.py:30
  49.4 1.6 fusion.4
  51.1 0.7 add_select_fusion.6
  51.8 74.6 %all-gather.5.cloned.1.call-done = f32[512,2048]{1,0:T(8,128)} async-done(((f32[128,2048]{1,0:T(8,128)}), f32[512,2048]{1,0:T(8,128)}) %all-gather.5.cloned.1.call-update) | async-done | bytes 4194320 | tf_op jit(solution)/shard_map/all_gather | solution.py:171
  126.4 4.6 %copy.8 = f32[4,8,16,2048]{3,2,0,1:T(8,128)} copy(f32[4,8,16,2048]{3,2,1,0:T(8,128)} %bitcast.6) | data formatting | bytes 8388608 | tf_op jit(solution)/shard_map/reshape | solution.py:173
  131.0 50.0 %all-gather.3.cloned.1.call-done = f32[512,4096]{1,0:T(8,128)} async-done(((f32[64,4096]{1,0:T(8,128)}), f32[512,4096]{1,0:T(8,128)}) %all-gather.3.cloned.1.call-update) | async-done | bytes 8388624 | tf_op jit(solution)/shard_map/all_gather | solution.py:175
  181.1 51.7 %add_add_fusion = f32[4096,2048]{1,0:T(8,128)} fusion(f32[4096]{0:T(1024)S(1)} %fusion.4, s32[2048]{0:T(1024)S(1)} %get-tuple-element.22, f32[2048]{0:T(1024)S(1)} %dynamic_slice.15, f32[4096]{0:T(1024)S(1)} %dynamic_slice.14, s32[2048]{0:T(1024)S(1)} %get-tuple-element.21, s32[2048]{0:T(1024)S(1)} %add_select_fusion.6, s32[4096]{0:T(1024)S(1)} %get-tuple-element.11, ...), kind=kOutput, calls=%fused_computation | convolution fusion | flops 25895632896 | bytes 46276608 | tf_op jit(solution)/shard_map/dot_general | solution.py:13
  (4 shorter events, 0.0 us)
Async XLA Ops:
  6.5 119.9 %all-gather.5.cloned.1.call-start = ((), (), s32[]{:S(2)}) async-start(), calls=%async_computation.1 | async-start | bytes 5242880 | tf_op jit(solution)/shard_map/all_gather | solution.py:171
  41.5 139.6 %all-gather.3.cloned.1.call-start = ((), (), s32[]{:S(2)}) async-start(), calls=%async_computation | async-start | bytes 9437184 | tf_op jit(solution)/shard_map/all_gather | solution.py:175
Sparse Core Ops, SparseCore 0:
  41.6 84.7 all-gather.4
  128.3 52.7 all-gather.2
